TPU v7x, 32 devices: a whole 2x2x4 slice. The times are simulated.
32 devices in a mesh: wide: 8 (over y, x, core), narrow: 4 (over z).
Axes of the slice: x: 2, y: 2, z: 4, core: 2. Of those that a mesh axis runs over, the one named last changes fastest.
Arguments:
- coefficients: float32 [8, 8192, 8192], P(None, 'wide', 'narrow'), may hold values from -0.07 to 0.07
- tensor_blocks: float32 [8, 32, 8192], P(None, 'wide', 'narrow'), may hold values from -6 to 6
- basis_rows: float32 [32, 8192], P(None, ('wide', 'narrow')), may hold values from -1.1 to 1.1, as said below
Outputs:
- new_basis: float32 [32, 8192], P(None, ('wide', 'narrow'))
- projection: float32 [32, 32], replicated
- factor: float32 [32, 32], replicated
Inputs may be any that keep to these rules, and one draw needn't show every extreme that they name: The rows of basis_rows are nearly but not exactly orthonormal: basis_rows basis_rows^T differs from the identity by less than 0.2 in spectral norm.
All inputs are finite; a program needn't handle non-finite values.
Results may differ from a plain program's by a relative error of at most 0.0002.
Values sent between devices are 32-bit elements; how exact they have to be, the bound alone decides.
A program may use at most 128 MiB of HBM per device.

v0:
```python
import jax
import jax.numpy as jnp
from jax import lax
from jax.sharding import PartitionSpec as P

N = 8192


def body(coefficients, tensor_blocks, basis_rows):
    hi = lax.Precision.HIGHEST
    partial_block = jnp.einsum(
        "kic,krc->ir",
        lax.all_gather(tensor_blocks, "wide", axis=1, tiled=True),
        coefficients,
        precision=hi,
    )
    image = lax.psum_scatter(partial_block, "narrow", scatter_dimension=1, tiled=True)
    local_first = jnp.dot(basis_rows, image.T, precision=hi)
    local_correlation = jnp.dot(basis_rows, basis_rows.T, precision=hi)
    first, correlation = lax.psum((local_first, local_correlation), ("wide", "narrow"))
    once = image - jnp.dot(first.T, basis_rows, precision=hi)
    second, raw_gram = lax.psum(
        (jnp.dot(basis_rows, once.T, precision=hi), jnp.dot(once, once.T, precision=hi)),
        ("wide", "narrow"),
    )
    twice = once - jnp.dot(second.T, basis_rows, precision=hi)
    cross = jnp.dot(second.T, second, precision=hi)
    weighted = jnp.dot(second.T, jnp.dot(correlation, second, precision=hi), precision=hi)
    gram = (raw_gram - 2.0 * cross + weighted) / N
    factor = jnp.linalg.cholesky(gram)
    new_basis = lax.linalg.triangular_solve(factor, twice, left_side=True, lower=True)
    return (new_basis, first + second, factor)


def solution(mesh):
    in_specs = (P(None, "wide", "narrow"), P(None, "wide", "narrow"), P(None, ("wide", "narrow")))
    out_specs = (P(None, ("wide", "narrow")), P(), P())
    return jax.shard_map(body, mesh=mesh, in_specs=in_specs, out_specs=out_specs, check_vma=False)
```

profile of v0, /device:TPU:0, one launch (start us, length us, event | category | flops | bytes accessed | tf_op | source)
XLA Modules:
  0.0 225.5 jit_solution(1987830653347588551)
XLA Ops:
  7.2 0.0 copy-start
  7.2 0.0 all-gather.2.cloned.1.call-start
  7.2 1.8 copy.11
  9.1 0.0 all-gather.2.cloned.1.call-update
  9.1 0.0 reduce-scatter.2.cloned.1.call-start
  9.1 31.3 %all-gather.2.cloned.1.call-done = f32[8,32,2048]{2,0,1:T(8,128)} async-done(((f32[8,4,2048]{2,0,1:T(8,128)}), f32[8,32,2048]{2,0,1:T(8,128)}) %all-gather.2.cloned.1.call-update) | async-done | bytes 2097168 | tf_op jit(solution)/shard_map/all_gather | solution.py:13
  40.4 67.1 %fusion.2 = f32[32,1024]{1,0:T(8,128)} fusion(f32[8,1024,2048]{2,1,0:T(8,128)} %param.3, f32[8,32,2048]{2,0,1:T(8,128)} %all-gather.2.cloned.1.call-done), kind=kOutput, calls=%fused_computation.2 | convolution fusion | flops 6442450944 | bytes 69337088 | tf_op jit(solution)/shard_map/kic,krc->ir/dot_general | solution.py:11
  107.5 0.0 reduce-scatter.2.cloned.1.call-update
  107.5 0.0 copy-done
  107.5 0.2 fusion.11
  107.7 19.4 %reduce-scatter.2.cloned.1.call-done = f32[32,256]{1,0:T(8,128)} async-done(((f32[32,1024]{1,0:T(8,128)}), f32[32,256]{1,0:T(8,128)}) %reduce-scatter.2.cloned.1.call-update) | async-done | bytes 32784 | tf_op jit(solution)/shard_map/reduce_scatter | solution.py:17
  127.1 0.9 convolution_bitcast_fusion.1
  128.1 38.5 %psum.28 = f32[32,32]{0,1:T(8,128)S(1)} all-reduce(f32[32,32]{0,1:T(8,128)S(1)} %convolution_bitcast_fusion.1), channel_id=1, replica_groups=mesh['wide'=8,'narrow'=4] {'wide','narrow'}, use_global_device_ids=true, to_apply=%region_1.0 | all-reduce | flops 1024 | bytes 8192 | tf_op jit(solution)/shard_map/psum | solution.py:20
  166.5 0.9 convolution_subtract_fusion.1
  167.4 0.2 convolution_bitcast_fusion
  167.6 0.2 fusion.10
  167.8 41.3 %all-reduce = (f32[32,32]{0,1:T(8,128)S(1)}, f32[32,32]{0,1:T(8,128)S(1)}, f32[32,32]{1,0:T(8,128)S(1)}) all-reduce(f32[32,32]{0,1:T(8,128)S(1)} %convolution_bitcast_fusion, f32[32,32]{0,1:T(8,128)S(1)} %fusion.10, f32[32,32]{1,0:T(8,128)S(1)} %fusion.11), channel_id=1, replica_groups=mesh['wide'=8,'narrow'=4] {'wide','narrow'}, use_global_device_ids=true, to_apply=%region_3.0 | all-reduce | flops 3072 | bytes 24576 | tf_op jit(solution)/shard_map/psum | solution.py:22
  209.1 0.2 convolution_subtract_fusion
  209.2 0.1 fusion.12
  209.4 0.2 fusion.6
  209.6 0.2 fusion.5
  209.8 0.1 copy.16
  209.9 2.9 %cholesky.16 = f32[32,32]{1,0:T(8,128)S(1)} custom-call(f32[32,32]{1,0:T(8,128)S(1)} %fusion.9), custom_call_target="Cholesky" | custom-call | tf_op jit(solution)/shard_map/jit(cholesky)/cholesky | solution.py:30
  212.8 0.6 compare_reduce_fusion
  213.5 1.3 select_bitcast_fusion
  214.7 2.4 %custom-call.6 = f32[1,32,32]{1,2,0:T(8,128)S(1)} custom-call(f32[1,32,32]{2,1,0:T(8,128)S(1)} %get-tuple-element.12), custom_call_target="InvertDiagBlocksLowerTriangular" | custom-call | tf_op jit(solution)/shard_map/triangular_solve | solution.py:31
  217.1 0.7 copy.17
  217.9 0.8 fusion.7
  (3 shorter events, 0.0 us)
Async XLA Ops:
  7.2 100.4 %copy-start = (f32[32,256]{1,0:T(8,128)S(1)}, f32[32,256]{1,0:T(8,128)}, u32[]{:S(2)}) copy-start(f32[32,256]{1,0:T(8,128)} %param.5) | copy-start | bytes 98308
  7.2 33.2 %all-gather.2.cloned.1.call-start = ((), (), s32[]{:S(2)}) async-start(), calls=%async_computation.1 | async-start | bytes 2359296 | tf_op jit(solution)/shard_map/all_gather | solution.py:13
  9.1 118.1 %reduce-scatter.2.cloned.1.call-start = ((), (), s32[]{:S(2)}) async-start(), calls=%async_computation.2 | async-start | bytes 163840 | tf_op jit(solution)/shard_map/reduce_scatter | solution.py:17
Sparse Core Ops, SparseCore 0:
  9.9 30.4 all-gather.1
  107.7 19.4 reduce-scatter.1
where the time goes:
time: 226 us
  blocking collectives  79.7 us (35%)
  matrix products  70.9 us (31%)
  waiting for transfers between devices  50.7 us (22%)
  between operations  14.1 us (6%)
  other arithmetic  7.3 us (3%)
  local copies, waits for them, and re-layouts  2.62 us (1%)
    dot_general x1, matrix products, body(): jnp.einsum('kic,krc->ir', lax.all_gather(tensor_blocks, 'wide', axis=1, t...  67.1 us
    psum x1, blocking collectives, body(): lax.psum((jnp.dot(basis_rows, once.T, precision=hi), jnp.dot(once, once.T...  41.3 us
    psum x1, blocking collectives, body(): lax.psum((local_first, local_correlation), ('wide', 'narrow'))  38.5 us
    all_gather x1, waiting for transfers between devices, body(): lax.all_gather(tensor_blocks, 'wide', axis=1, tiled=True)  31.3 us
    reduce_scatter x1, waiting for transfers between devices, body(): lax.psum_scatter(partial_block, 'narrow', scatter_dimension=1, tiled=True)  19.4 us
  transfers between devices with their start and end apart: 2, of which 2 were waited for; matrix products, arithmetic and copies ran while one was open for 0% of the time, Pallas kernels for 0%

commit v1 on v0

--- a/solution.py
+++ b/solution.py
@@ -6,13 +6,23 @@
 N = 8192
 
 
+def ring_gather(x, axis, dim):
+    ways = lax.axis_size(axis)
+    up = [(d, (d + 1) % ways) for d in range(ways)]
+    down = [(d, (d - 1) % ways) for d in range(ways)]
+    earlier, later = ([x], [x])
+    for _ in range(ways // 2):
+        earlier.append(lax.ppermute(earlier[-1], axis, up))
+    for _ in range((ways - 1) // 2):
+        later.append(lax.ppermute(later[-1], axis, down))
+    line = jnp.concatenate([*earlier[::-1], *later[1:]], axis=dim)
+    return jnp.roll(line, (lax.axis_index(axis) - ways // 2) * x.shape[dim], axis=dim)
+
+
 def body(coefficients, tensor_blocks, basis_rows):
     hi = lax.Precision.HIGHEST
     partial_block = jnp.einsum(
-        "kic,krc->ir",
-        lax.all_gather(tensor_blocks, "wide", axis=1, tiled=True),
-        coefficients,
-        precision=hi,
+        "kic,krc->ir", ring_gather(tensor_blocks, "wide", 1), coefficients, precision=hi
     )
     image = lax.psum_scatter(partial_block, "narrow", scatter_dimension=1, tiled=True)
     local_first = jnp.dot(basis_rows, image.T, precision=hi)

time: 226 us -> 237 us (1.049)
  starting transfers between devices: 0.08 us -> 9.96 us
  local copies, waits for them, and re-layouts: 2.62 us -> 10 us
  waiting for transfers between devices: 50.7 us -> 44.9 us
    all_gather x1 -> x0, waiting for transfers between devices: 31.3 us -> none  [body(): lax.all_gather(tensor_blocks, 'wide', axis=1, tiled=True)]
    ppermute x0 -> x7, waiting for transfers between devices: none -> 19.1 us  [the longest x4 15.1 us: ring_gather(): earlier.append(lax.ppermute(earlier[-1], axis, up))]
    ppermute x0 -> x7, starting transfers between devices: none -> 9.92 us  [the longest x3 8.44 us: ring_gather(): later.append(lax.ppermute(later[-1], axis, down))]
    concatenate x0 -> x1, local copies, waits for them, and re-layouts: none -> 9.22 us  [ring_gather(): jnp.roll(line, (lax.axis_index(axis) - ways // 2) * x.shape[dim], axis=dim)]
    reduce_scatter x1, waiting for transfers between devices: 19.4 us -> 25.8 us  [body(): lax.psum_scatter(partial_block, 'narrow', scatter_dimension=1, tiled=True)]
  transfers between devices with their start and end apart: 2 -> 8, of which waited for: 2 -> 8; matrix products, arithmetic and copies ran while one was open for 0% -> 0% of each run, Pallas kernels for 0% -> 0%
where the time goes in v1:
time: 237 us
  blocking collectives  80 us (34%)
  matrix products  70.6 us (30%)
  waiting for transfers between devices  44.9 us (19%)
  between operations  14.1 us (6%)
  local copies, waits for them, and re-layouts  10 us (4%)
  starting transfers between devices  9.96 us (4%)
  other arithmetic  7.3 us (3%)
    dot_general x1, matrix products, body(): jnp.einsum('kic,krc->ir', ring_gather(tensor_blocks, 'wide', 1), coeffici...  66.8 us
    psum x1, blocking collectives, body(): lax.psum((jnp.dot(basis_rows, once.T, precision=hi), jnp.dot(once, once.T...  41.3 us
    psum x1, blocking collectives, body(): lax.psum((local_first, local_correlation), ('wide', 'narrow'))  38.6 us
    reduce_scatter x1, waiting for transfers between devices, body(): lax.psum_scatter(partial_block, 'narrow', scatter_dimension=1, tiled=True)  25.8 us
    ppermute x4, waiting for transfers between devices, ring_gather(): earlier.append(lax.ppermute(earlier[-1], axis, up))  15.1 us
    concatenate x1, local copies, waits for them, and re-layouts, ring_gather(): jnp.roll(line, (lax.axis_index(axis) - ways // 2) * x.shape[dim], axis=dim)  9.22 us
    ppermute x3, starting transfers between devices, ring_gather(): later.append(lax.ppermute(later[-1], axis, down))  8.44 us
  transfers between devices with their start and end apart: 8, of which 8 were waited for; matrix products, arithmetic and copies ran while one was open for 0% of the time, Pallas kernels for 0%

profile of v1, /device:TPU:0, one launch (start us, length us, event | category | flops | bytes accessed | tf_op | source)
XLA Modules:
  0.0 236.9 jit_solution(6023004339259775692)
XLA Ops:
  7.2 0.5 collective-permute-start
  7.8 2.9 %collective-permute-start.4 = (f32[8,4,2048]{2,1,0:T(4,128)}, f32[8,4,2048]{2,1,0:T(4,128)S(1)}, u32[]{:S(2)}, u32[]{:S(2)}) collective-permute-start(f32[8,4,2048]{2,1,0:T(4,128)} %param.4), channel_id=1, source_target_pairs={{0,28},{4,0},{8,4},{12,8},{16,12},{20,16},{24,20},{28,24},{1,29},{... | collective-permute-start | bytes 786440 | tf_op jit(solution)/shard_map/ppermute | solution.py:17
  10.7 4.4 %collective-permute-done = f32[8,4,2048]{2,1,0:T(4,128)S(1)} collective-permute-done((f32[8,4,2048]{2,1,0:T(4,128)}, f32[8,4,2048]{2,1,0:T(4,128)S(1)}, u32[]{:S(2)}, u32[]{:S(2)}) %collective-permute-start) | collective-permute-done | bytes 262176 | tf_op jit(solution)/shard_map/ppermute | solution.py:15
  15.1 0.6 collective-permute-start.1
  15.8 0.9 collective-permute-done.4
  16.7 2.7 %collective-permute-start.5 = (f32[8,4,2048]{2,1,0:T(4,128)S(1)}, f32[8,4,2048]{2,1,0:T(4,128)S(1)}, u32[]{:S(2)}, u32[]{:S(2)}) collective-permute-start(f32[8,4,2048]{2,1,0:T(4,128)S(1)} %collective-permute-done.4), channel_id=1, source_target_pairs={{0,28},{4,0},{8,4},{12,8},{16,12},{20,16},{24,20},{28,24},{1,29},{... | collective-permute-start | bytes 786440 | tf_op jit(solution)/shard_map/ppermute | solution.py:17
  19.4 2.7 %collective-permute-done.1 = f32[8,4,2048]{2,1,0:T(4,128)S(1)} collective-permute-done((f32[8,4,2048]{2,1,0:T(4,128)S(1)}, f32[8,4,2048]{2,1,0:T(4,128)S(1)}, u32[]{:S(2)}, u32[]{:S(2)}) %collective-permute-start.1) | collective-permute-done | bytes 262176 | tf_op jit(solution)/shard_map/ppermute | solution.py:15
  22.0 0.3 collective-permute-start.2
  22.3 1.8 collective-permute-done.5
  24.1 2.8 %collective-permute-start.6 = (f32[8,4,2048]{2,1,0:T(4,128)S(1)}, f32[8,4,2048]{2,1,0:T(4,128)S(1)}, u32[]{:S(2)}, u32[]{:S(2)}) collective-permute-start(f32[8,4,2048]{2,1,0:T(4,128)S(1)} %collective-permute-done.5), channel_id=1, source_target_pairs={{0,28},{4,0},{8,4},{12,8},{16,12},{20,16},{24,20},{28,24},{1,29},{... | collective-permute-start | bytes 786440 | tf_op jit(solution)/shard_map/ppermute | solution.py:17
  27.0 2.6 %collective-permute-done.2 = f32[8,4,2048]{2,1,0:T(4,128)S(1)} collective-permute-done((f32[8,4,2048]{2,1,0:T(4,128)S(1)}, f32[8,4,2048]{2,1,0:T(4,128)S(1)}, u32[]{:S(2)}, u32[]{:S(2)}) %collective-permute-start.2) | collective-permute-done | bytes 262176 | tf_op jit(solution)/shard_map/ppermute | solution.py:15
  29.6 1.3 collective-permute-done.6
  30.8 5.4 %collective-permute-done.3 = f32[8,4,2048]{2,1,0:T(4,128)S(1)} collective-permute-done((f32[8,4,2048]{2,1,0:T(4,128)S(1)}, f32[8,4,2048]{2,1,0:T(4,128)S(1)}, u32[]{:S(2)}, u32[]{:S(2)}) %collective-permute-start.3) | collective-permute-done | bytes 262176 | tf_op jit(solution)/shard_map/ppermute | solution.py:15
  36.3 9.2 %concatenate.6 = f32[8,64,2048]{2,1,0:T(8,128)} concatenate(f32[8,4,2048]{2,1,0:T(4,128)S(1)} %collective-permute-done.3, f32[8,4,2048]{2,1,0:T(4,128)S(1)} %collective-permute-done.2, f32[8,4,2048]{2,1,0:T(4,128)S(1)} %collective-permute-done.1, f32[8,4,2048]{2,1,0:T(4,128)S(1)} %collective-permute-done, f32[8,4,2048]{2,1,0:T(4,128)} %param.4, ...), dimensions={1} | concatenate | bytes 8388608 | tf_op jit(solution)/shard_map/jit(_roll_dynamic)/concatenate | solution.py:19
  45.5 66.8 %fusion.2 = f32[32,1024]{1,0:T(8,128)} fusion(f32[8,1024,2048]{2,1,0:T(8,128)} %param.3, f32[8,64,2048]{2,1,0:T(8,128)} %concatenate.6, s32[]{:T(128)S(6)} %select_n.18), kind=kOutput, calls=%fused_computation.2 | convolution fusion | flops 6442450944 | bytes 69337088 | tf_op jit(solution)/shard_map/kic,krc->ir/dot_general | solution.py:24
  112.3 0.2 fusion.12
  112.5 25.8 %reduce-scatter.2.cloned.1.call-done = f32[32,256]{1,0:T(8,128)} async-done(((f32[32,1024]{1,0:T(8,128)}), f32[32,256]{1,0:T(8,128)}) %reduce-scatter.2.cloned.1.call-update) | async-done | bytes 32784 | tf_op jit(solution)/shard_map/reduce_scatter | solution.py:27
  138.3 0.9 convolution_bitcast_fusion.1
  139.2 38.6 %psum.28 = f32[32,32]{0,1:T(8,128)S(1)} all-reduce(f32[32,32]{0,1:T(8,128)S(1)} %convolution_bitcast_fusion.1), channel_id=1, replica_groups=mesh['wide'=8,'narrow'=4] {'wide','narrow'}, use_global_device_ids=true, to_apply=%region_1.2 | all-reduce | flops 1024 | bytes 8192 | tf_op jit(solution)/shard_map/psum | solution.py:30
  177.8 0.9 convolution_subtract_fusion.1
  178.8 0.2 convolution_bitcast_fusion
  178.9 0.2 fusion.11
  179.1 41.3 %all-reduce = (f32[32,32]{0,1:T(8,128)S(1)}, f32[32,32]{0,1:T(8,128)S(1)}, f32[32,32]{1,0:T(8,128)S(1)}) all-reduce(f32[32,32]{0,1:T(8,128)S(1)} %convolution_bitcast_fusion, f32[32,32]{0,1:T(8,128)S(1)} %fusion.11, f32[32,32]{1,0:T(8,128)S(1)} %fusion.12), channel_id=1, replica_groups=mesh['wide'=8,'narrow'=4] {'wide','narrow'}, use_global_device_ids=true, to_apply=%region_3.4 | all-reduce | flops 3072 | bytes 24576 | tf_op jit(solution)/shard_map/psum | solution.py:32
  220.4 0.2 convolution_subtract_fusion
  220.6 0.1 fusion.6
  220.9 0.2 fusion.5
  221.2 2.9 %cholesky.16 = f32[32,32]{1,0:T(8,128)S(1)} custom-call(f32[32,32]{1,0:T(8,128)S(1)} %fusion.9), custom_call_target="Cholesky" | custom-call | tf_op jit(solution)/shard_map/jit(cholesky)/cholesky | solution.py:40
  224.2 0.6 compare_reduce_fusion
  224.8 1.3 select_bitcast_fusion
  226.1 2.4 %custom-call.6 = f32[1,32,32]{1,2,0:T(8,128)S(1)} custom-call(f32[1,32,32]{2,1,0:T(8,128)S(1)} %get-tuple-element.9), custom_call_target="InvertDiagBlocksLowerTriangular" | custom-call | tf_op jit(solution)/shard_map/triangular_solve | solution.py:41
  228.5 0.7 copy.10
  229.2 0.8 fusion.7
  (10 shorter events, 0.3 us)
Async XLA Ops:
  7.2 105.2 %copy-start = (f32[32,256]{1,0:T(8,128)S(1)}, f32[32,256]{1,0:T(8,128)}, u32[]{:S(2)}) copy-start(f32[32,256]{1,0:T(8,128)} %param.5) | copy-start | bytes 98308
  7.2 131.1 %reduce-scatter.2.cloned.1.call-start = ((), (), s32[]{:S(2)}) async-start(), calls=%async_computation.1 | async-start | bytes 163840 | tf_op jit(solution)/shard_map/reduce_scatter | solution.py:27
  7.2 7.9 %collective-permute-start = (f32[8,4,2048]{2,1,0:T(4,128)}, f32[8,4,2048]{2,1,0:T(4,128)S(1)}, u32[]{:S(2)}, u32[]{:S(2)}) collective-permute-start(f32[8,4,2048]{2,1,0:T(4,128)} %param.4), channel_id=1, source_target_pairs={{0,4},{4,8},{8,12},{12,16},{16,20},{20,24},{24,28},{28,0},{1,5},{5... | collective-permute-start | bytes 786440 | tf_op jit(solution)/shard_map/ppermute | solution.py:15
  7.8 8.9 %collective-permute-start.4 = (f32[8,4,2048]{2,1,0:T(4,128)}, f32[8,4,2048]{2,1,0:T(4,128)S(1)}, u32[]{:S(2)}, u32[]{:S(2)}) collective-permute-start(f32[8,4,2048]{2,1,0:T(4,128)} %param.4), channel_id=1, source_target_pairs={{0,28},{4,0},{8,4},{12,8},{16,12},{20,16},{24,20},{28,24},{1,29},{... | collective-permute-start | bytes 786440 | tf_op jit(solution)/shard_map/ppermute | solution.py:17
  15.1 6.9 %collective-permute-start.1 = (f32[8,4,2048]{2,1,0:T(4,128)S(1)}, f32[8,4,2048]{2,1,0:T(4,128)S(1)}, u32[]{:S(2)}, u32[]{:S(2)}) collective-permute-start(f32[8,4,2048]{2,1,0:T(4,128)S(1)} %collective-permute-done), channel_id=1, source_target_pairs={{0,4},{4,8},{8,12},{12,16},{16,20},{20,24},{24,28},{28,0},{1,5},{5... | collective-permute-start | bytes 786440 | tf_op jit(solution)/shard_map/ppermute | solution.py:15
  16.7 7.5 %collective-permute-start.5 = (f32[8,4,2048]{2,1,0:T(4,128)S(1)}, f32[8,4,2048]{2,1,0:T(4,128)S(1)}, u32[]{:S(2)}, u32[]{:S(2)}) collective-permute-start(f32[8,4,2048]{2,1,0:T(4,128)S(1)} %collective-permute-done.4), channel_id=1, source_target_pairs={{0,28},{4,0},{8,4},{12,8},{16,12},{20,16},{24,20},{28,24},{1,29},{... | collective-permute-start | bytes 786440 | tf_op jit(solution)/shard_map/ppermute | solution.py:17
  22.0 7.5 %collective-permute-start.2 = (f32[8,4,2048]{2,1,0:T(4,128)S(1)}, f32[8,4,2048]{2,1,0:T(4,128)S(1)}, u32[]{:S(2)}, u32[]{:S(2)}) collective-permute-start(f32[8,4,2048]{2,1,0:T(4,128)S(1)} %collective-permute-done.1), channel_id=1, source_target_pairs={{0,4},{4,8},{8,12},{12,16},{16,20},{20,24},{24,28},{28,0},{1,5},{5... | collective-permute-start | bytes 786440 | tf_op jit(solution)/shard_map/ppermute | solution.py:15
  24.1 6.7 %collective-permute-start.6 = (f32[8,4,2048]{2,1,0:T(4,128)S(1)}, f32[8,4,2048]{2,1,0:T(4,128)S(1)}, u32[]{:S(2)}, u32[]{:S(2)}) collective-permute-start(f32[8,4,2048]{2,1,0:T(4,128)S(1)} %collective-permute-done.5), channel_id=1, source_target_pairs={{0,28},{4,0},{8,4},{12,8},{16,12},{20,16},{24,20},{28,24},{1,29},{... | collective-permute-start | bytes 786440 | tf_op jit(solution)/shard_map/ppermute | solution.py:17
  29.6 6.7 %collective-permute-start.3 = (f32[8,4,2048]{2,1,0:T(4,128)S(1)}, f32[8,4,2048]{2,1,0:T(4,128)S(1)}, u32[]{:S(2)}, u32[]{:S(2)}) collective-permute-start(f32[8,4,2048]{2,1,0:T(4,128)S(1)} %collective-permute-done.2), channel_id=1, source_target_pairs={{0,4},{4,8},{8,12},{12,16},{16,20},{20,24},{24,28},{28,0},{1,5},{5... | collective-permute-start | bytes 786440 | tf_op jit(solution)/shard_map/ppermute | solution.py:15
Sparse Core Ops, SparseCore 0:
  112.5 25.7 reduce-scatter.1
